TPU v7x, 256 devices: a 2x2x32 block of a 4x8x32 slice. The times are simulated.
256 devices in a mesh: groups: 4 (over x, y), seq: 32 (over z), pd: 2 (over core).
Axes of the slice: x: 2, y: 2, z: 32, core: 2. Of those that a mesh axis runs over, the one named last changes fastest.
The devices are a block of a 4x8x32 slice.
Arguments:
- streams: bfloat16 [32768, 4, 7168], P(('groups', 'seq'), None, 'pd'), parts along dimension 0, may hold values from -6 to 6
- mix_first: bfloat16 [4, 7168, 24], P(None, 'pd'), may hold values from -0.03125 to 0.03125
- first_layer_bias: float32 [24], replicated, may hold values from -3 to 3
- pre_second: bfloat16 [4, 7168, 4], P(None, 'pd'), may hold values from -0.03125 to 0.03125
- bias_second: float32 [4], replicated, may hold values from -3 to 3
- w_latent: bfloat16 [2, 7168, 576], P(None, ('pd', 'seq')), may hold values from -0.0625 to 0.0625
- latent_gain: float32 [2, 512], replicated, may hold values from 0.5 to 1.5
- out_weight: bfloat16 [512, 7168], P(None, 'pd'), may hold values from -0.25 to 0.25
- span_slot: int32 [256], P('groups'), parts along dimension 0, may hold values from 0 to 63, each once
- block_owner: int32 [128], P('groups'), parts along dimension 0, may hold values from 0 to 31, each once
- prompt_length: int32 [4], P('groups'), parts along dimension 0, may hold values from 4096 to 8192
Outputs:
- cache: bfloat16 [2, 32768, 576], P(None, ('groups', 'seq')), parts along dimension 1
There are 4 independent parts, one for each index of `groups`. A program takes and returns all parts, laid end to end along the dimension named above; an argument that names none is the same for every part. Nothing has to cross between parts.
Inputs may be any that keep to these rules, and one draw needn't show every extreme that they name: span_slot is a permutation; slot q lies in rows q * 128 to q * 128 + 127 of streams. block_owner is a permutation.
All inputs are finite; a program needn't handle non-finite values.
Results may differ from a plain program's by a relative error of at most 0.0058.
Values may be sent and summed in bfloat16 or wider, within the bound.
A program may use at most 128 MiB of HBM per device.

v0:
```python
import jax
import jax.numpy as jnp
from jax import lax
from jax.sharding import PartitionSpec as P

LAT = 512
ROPE = 64
RESIDUAL_WAYS = 4
SINK = 20
EPSILON = 1e-06
THETA = 10000.0


def sent_to_all(x, axis):
    copies = jnp.broadcast_to(x, (lax.axis_size(axis), *x.shape))
    return lax.all_to_all(copies, axis, split_axis=0, concat_axis=0, tiled=True)


def taken_together(x, axis):
    return sent_to_all(x, axis).sum(axis=0)


def packed_total(arrays, axis):
    ends = [0]
    for a in arrays:
        ends.append(ends[-1] + a.size)
    so_far = taken_together(jnp.concatenate([a.ravel() for a in arrays]), axis)
    return tuple((so_far[b:e].reshape(a.shape) for a, b, e in zip(arrays, ends, ends[1:])))


def doubly_stochastic_normalize(blend_scores_raw):

    def one_sweep(turn_index, matrix):
        matrix = matrix / jnp.sum(matrix, axis=2, keepdims=True)
        return matrix / jnp.sum(matrix, axis=1, keepdims=True)

    return lax.fori_loop(0, SINK, one_sweep, jnp.exp(blend_scores_raw))


def combine(weights, stream_block):
    weighted = weights[:, 0, None] * stream_block[:, 0, :].astype(jnp.float32)
    for stream_index in range(1, RESIDUAL_WAYS):
        weighted = weighted + weights[:, stream_index, None] * stream_block[
            :, stream_index, :
        ].astype(jnp.float32)
    return weighted


def coefficients(stream_block, weights, offsets):
    flattened = stream_block.reshape(stream_block.shape[0], -1)
    partial_value = jnp.dot(
        flattened, weights.reshape(flattened.shape[1], -1), preferred_element_type=jnp.float32
    )
    elementwise_power_two = jnp.sum(jnp.square(flattened.astype(jnp.float32)), axis=1)
    projected, square_sum = packed_total((partial_value, elementwise_power_two), "pd")
    entry_count = flattened.shape[1] * lax.axis_size("pd")
    rms_scale = jnp.sqrt(square_sum / entry_count + EPSILON)
    return projected / rms_scale[:, None] + offsets[None, :]


def cache_entry(summed, places, gain_row):
    latent = summed[:, :LAT]
    mean_square = jnp.mean(latent * latent, axis=1, keepdims=True)
    normed = latent * lax.rsqrt(mean_square + EPSILON) * gain_row[None, :]
    half_rope = ROPE // 2
    frequency = THETA ** (-jnp.arange(half_rope, dtype=jnp.float32) / half_rope)
    angles = places.astype(jnp.float32)[:, None] * frequency[None, :]
    first_half = summed[:, LAT : LAT + half_rope]
    second = summed[:, LAT + half_rope :]
    cosine_table = jnp.cos(angles)
    sine_values = jnp.sin(angles)
    rotated = jnp.concatenate(
        [
            first_half * cosine_table - second * sine_values,
            second * cosine_table + first_half * sine_values,
        ],
        axis=1,
    )
    return jnp.concatenate([normed, rotated], axis=1).astype(jnp.bfloat16)


def on_device(
    streams,
    mix_first,
    first_layer_bias,
    pre_second,
    bias_second,
    w_latent,
    latent_gain,
    out_weight,
    span_slot,
    block_owner,
    prompt_length,
):
    tokens_here = streams.shape[0]
    span_rows = tokens_here // 2
    seq_count = lax.axis_size("seq")
    my_index = lax.axis_index("seq")
    own_slots = 2 * my_index + jnp.arange(2, dtype=jnp.int32)
    span_ids = jnp.arange(2 * seq_count, dtype=jnp.int32)
    own_spans = jnp.sum(
        span_ids[None, :] * (span_slot[None, :] == own_slots[:, None]).astype(jnp.int32), axis=1
    )
    places = (
        own_spans[:, None] * span_rows + jnp.arange(span_rows, dtype=jnp.int32)[None, :]
    ).reshape(-1)
    in_prompt = places < prompt_length[0]
    my_block = jnp.sum(
        jnp.arange(seq_count, dtype=jnp.int32) * (block_owner == my_index).astype(jnp.int32)
    )
    wanted_slots = span_slot[2 * my_block + jnp.arange(2, dtype=jnp.int32)]

    def latent_of(hidden, layer_index):
        partial_value = jnp.dot(
            hidden,
            lax.all_gather(w_latent[layer_index], "seq", axis=0, tiled=True),
            preferred_element_type=jnp.float32,
        )
        summed = taken_together(partial_value, "pd")
        return cache_entry(summed, places, latent_gain[layer_index])

    def masked(entry_rows):
        return jnp.where(in_prompt[:, None], entry_rows, jnp.zeros((), jnp.bfloat16))

    blend_weight = coefficients(streams, mix_first, first_layer_bias)
    pre_gate = jax.nn.sigmoid(blend_weight[:, :RESIDUAL_WAYS])
    post_gate = 2.0 * jax.nn.sigmoid(blend_weight[:, RESIDUAL_WAYS : 2 * RESIDUAL_WAYS])
    residual_blend_matrix = doubly_stochastic_normalize(
        blend_weight[:, 2 * RESIDUAL_WAYS :].reshape(-1, RESIDUAL_WAYS, RESIDUAL_WAYS)
    )
    hidden = combine(pre_gate, streams).astype(jnp.bfloat16)
    entry_first = latent_of(hidden, 0)
    branch = jnp.dot(entry_first[:, :LAT], out_weight, preferred_element_type=jnp.float32)
    updated = jnp.stack(
        [
            combine(residual_blend_matrix[:, stream_index, :], streams)
            + post_gate[:, stream_index, None] * branch
            for stream_index in range(RESIDUAL_WAYS)
        ],
        axis=1,
    ).astype(jnp.bfloat16)
    second_coef = coefficients(updated, pre_second, bias_second)
    hidden_second = combine(jax.nn.sigmoid(second_coef), updated).astype(jnp.bfloat16)
    entry_second = latent_of(hidden_second, 1)
    stacked = jnp.stack([masked(entry_first), masked(entry_second)])
    collected = jnp.zeros_like(stacked)
    shard_piece = lax.all_gather(stacked, "seq", axis=1, tiled=True)
    piece_rows = shard_piece.shape[1]
    span_parts = []
    for lane in range(2):
        offset = wanted_slots[lane] * span_rows
        inside = jnp.logical_and(offset >= 0, offset + span_rows <= piece_rows)
        clipped = jnp.clip(offset, 0, piece_rows - span_rows)
        sliced = lax.dynamic_slice_in_dim(shard_piece, clipped, span_rows, 1)
        span_parts.append(
            jnp.where(inside, sliced, collected[:, lane * span_rows : (lane + 1) * span_rows])
        )
    return jnp.concatenate(span_parts, axis=1)


def solution(mesh):
    placed = (
        P(("groups", "seq"), None, "pd"),
        P(None, "pd", None),
        P(),
        P(None, "pd", None),
        P(),
        P(None, ("pd", "seq"), None),
        P(),
        P(None, "pd"),
        P("groups"),
        P("groups"),
        P("groups"),
    )
    return jax.shard_map(
        on_device,
        mesh=mesh,
        in_specs=placed,
        out_specs=P(None, ("groups", "seq"), None),
        check_vma=False,
    )
```

profile of v0, /device:TPU:38, one launch (start us, length us, event | category | flops | bytes accessed | tf_op | source)
XLA Modules:
  0.0 583.2 jit_solution(3354800891817134645)
XLA Ops:
  6.6 1.8 fusion.78
  8.4 5.2 convolution_bitcast_fusion
  13.6 0.1 reshape.292
  13.7 8.0 %multiply_reduce_fusion.1 = f32[256]{0:T(256)S(1)} fusion(bf16[256,4,3584]{2,1,0:T(4,128)(2,1)} %param.13), kind=kLoop, calls=%fused_computation.4 | loop fusion | flops 11009792 | bytes 7341056 | tf_op jit(solution)/shard_map/reduce_sum | solution.py:54
  21.7 0.6 broadcast_in_dim.23
  22.4 3.3 all-to-all-start
  25.8 0.7 all-gather.10.cloned.1.call-update
  26.6 0.5 all-to-all-done
  27.1 0.1 reduce_sum.111
  27.2 0.1 reshape.293
  27.4 0.1 divide_add_fusion
  27.5 1.7 while.10
  29.3 7.4 %copy.65 = bf16[256,4,3584]{2,0,1:T(8,128)(2,1)} copy(bf16[256,4,3584]{2,1,0:T(4,128)(2,1)} %param.13) | data formatting | bytes 14680064 | tf_op args[0]
  37.3 0.2 fusion.67
  37.5 0.1 compare_bitcast_fusion
  37.7 121.9 %all-gather.8.cloned.1.call-done = bf16[1,3584,576]{2,1,0:T(8,128)(2,1)} async-done(((bf16[1,112,576]{2,1,0:T(8,128)(2,1)}), bf16[1,3584,576]{2,1,0:T(8,128)(2,1)}) %all-gather.8.cloned.1.call-update) | async-done | bytes 4128784 | tf_op jit(solution)/shard_map/all_gather | solution.py:116
  159.6 8.4 %fusion.2 = f32[256,576]{0,1:T(8,128)S(1)} fusion(bf16[1,3584,576]{2,1,0:T(8,128)(2,1)} %all-gather.8.cloned.1.call-done, f32[256]{0:T(256)S(1)} %bitcast.168, f32[256]{0:T(256)S(1)} %bitcast.167, f32[256]{0:T(256)S(1)} %bitcast.166, f32[256]{0:T(256)S(1)} %bitcast.169, bf16[256,4,3584]{2,0,1:T(8,128)(2,1)} %copy.65), kind=kOutput, calls=%fused_computation.28 | convolution fusion | flops 1067974656 | bytes 12062720 | tf_op jit(solution)/shard_map/dot_general | solution.py:114
  168.0 0.1 broadcast_in_dim.24
  168.1 4.7 all_to_all.22
  172.8 0.1 reduce_sum.112
  173.0 0.1 multiply_reduce_fusion.3
  173.1 7.9 %fusion.12 = (bf16[256,3584]{1,0:T(8,128)(2,1)S(1)}, bf16[256,3584]{1,0:T(8,128)(2,1)S(1)}, f32[256,3584]{1,0:T(8,128)S(1)}) fusion(f32[256]{0:T(256)S(1)} %bitcast.160, f32[256]{0:T(256)S(1)} %bitcast.163, f32[256]{0:T(256)S(1)} %bitcast.164, f32[256]{0:T(256)S(1)} %bitcast.165, f32[256]{0:T(256)S(1)} %bitcast.162, bf16[256,4,3584]{2,0,1:T(8,128)(2,1)} %copy.65, ...), kind=kOutput, calls=%fused_computation.38 | convolution fusion | flops 961937408 | bytes 18887680 | tf_op jit(solution)/shard_map/dot_general | solution.py:133
  181.0 4.1 fusion.17
  185.2 1.2 copy-done.3
  186.4 2.0 fusion.38
  188.5 0.1 reshape.294
  188.6 4.0 multiply_reduce_fusion
  192.7 3.7 all_to_all.23
  196.4 0.1 reshape.295
  196.6 0.1 copy.75
  196.7 0.1 add_divide_fusion
  196.8 0.1 fusion.76
  196.9 95.3 %all-gather.10.cloned.1.call-done = bf16[1,3584,576]{2,1,0:T(8,128)(2,1)} async-done(((bf16[1,112,576]{2,1,0:T(8,128)(2,1)}), bf16[1,3584,576]{2,1,0:T(8,128)(2,1)}) %all-gather.10.cloned.1.call-update) | async-done | bytes 4128784 | tf_op jit(solution)/shard_map/all_gather | solution.py:116
  292.2 6.6 %fusion = f32[256,576]{0,1:T(8,128)S(1)} fusion(bf16[1,3584,576]{2,1,0:T(8,128)(2,1)} %all-gather.10.cloned.1.call-done, bf16[256,3584]{1,0:T(8,128)(2,1)} %copy-done.5, bf16[256,3584]{1,0:T(8,128)(2,1)} %copy-done.3, bf16[256,3584]{1,0:T(8,128)(2,1)S(1)} %get-tuple-element.28, bf16[256,3584]{1,0:T(8,128)(2,1)} %copy-done.4, f32[256]{0:T(256)S(1)} %bitcast.175, ...), kind=kOutput, calls=%fused_computation.26 | convolution fusion | flops 1067974656 | bytes 12062720 | tf_op jit(solution)/shard_map/dot_general | solution.py:114
  298.8 0.1 broadcast_in_dim.27
  298.9 4.7 all_to_all.24
  303.6 0.1 reduce_sum.116
  303.7 0.1 multiply_reduce_fusion.2
  303.8 0.1 fusion.39
  304.0 0.2 fusion.59
  304.2 0.1 maximum_select_fusion
  304.3 0.9 pad_maximum_fusion.4
  305.2 0.7 fusion.72
  306.7 0.6 gather_fusion
  307.3 0.6 fusion.87
  309.2 265.1 %all-gather.6.cloned.1.call-done = bf16[2,8192,576]{1,2,0:T(8,128)(2,1)} async-done(((bf16[2,256,576]{1,2,0:T(8,128)(2,1)}), bf16[2,8192,576]{1,2,0:T(8,128)(2,1)}) %all-gather.6.cloned.1.call-update) | async-done | bytes 18874384 | tf_op jit(solution)/shard_map/all_gather | solution.py:147
  574.3 1.5 dynamic-slice_select_fusion.1
  575.8 0.9 pad_maximum_fusion.5
  (117 shorter events, 1.9 us)
Async XLA Ops:
  6.5 1.9 copy-start
  6.6 153.1 %all-gather.8.cloned.1.call-start = ((), (), s32[]{:S(2)}) async-start(), calls=%async_computation.5 | async-start | bytes 4730880 | tf_op jit(solution)/shard_map/all_gather | solution.py:116
  13.7 13.6 %copy-start.7 = (f32[24]{0:T(128)S(1)}, f32[24]{0:T(128)}, u32[]{:S(2)}) copy-start(f32[24]{0:T(128)} %param.15) | copy-start | bytes 292
  22.4 4.7 all-to-all-start
  25.7 266.6 %all-gather.10.cloned.1.call-start = ((), (), s32[]{:S(2)}) async-start(), calls=%async_computation.6 | async-start | bytes 4730880 | tf_op jit(solution)/shard_map/all_gather | solution.py:116
  26.5 547.8 %all-gather.6.cloned.1.call-start = ((), (), s32[]{:S(2)}) async-start(), calls=%async_computation.4 | async-start | bytes 19464192 | tf_op jit(solution)/shard_map/all_gather | solution.py:147
  29.2 8.0 %copy-start.2 = (s32[64]{0:T(128)S(1)}, s32[64]{0:T(128)}, u32[]{:S(2)}) copy-start(s32[64]{0:T(128)} %param.21) | copy-start | bytes 772
  29.2 8.4 %copy-start.6 = (f32[2,512]{1,0:T(2,128)S(1)}, f32[2,512]{1,0:T(2,128)}, u32[]{:S(2)}) copy-start(f32[2,512]{1,0:T(2,128)} %param.19) | copy-start | bytes 12292
  173.1 7.9 %slice-start = ((s8[7340032]{0:T(1024)(128)(4,1)}), s8[4194304]{0:T(1024)(128)(4,1)S(1)}, s32[]{:S(2)}) async-start(s8[7340032]{0:T(1024)(128)(4,1)} %bitcast.137), calls=%async_computation.7 | async-start | bytes 8388608
  173.1 7.9 %slice-start.1 = ((s8[7340032]{0:T(1024)(128)(4,1)}), s8[3145728]{0:T(1024)(128)(4,1)S(1)}, s32[]{:S(2)}) async-start(s8[7340032]{0:T(1024)(128)(4,1)} %bitcast.137), calls=%async_computation.8 | async-start | bytes 6291456
  181.0 4.2 copy-start.4
  181.0 4.2 copy-start.5
  181.0 5.4 copy-start.9
  185.2 1.2 copy-start.3
  188.6 8.1 %copy-start.8 = (f32[4]{0:T(128)S(1)}, f32[4]{0:T(128)}, u32[]{:S(2)}) copy-start(f32[4]{0:T(128)} %param.17) | copy-start | bytes 52
  303.6 1.6 copy-start.10
  303.6 273.1 %copy-start.1 = (bf16[4,3584,24]{1,2,0:T(8,128)(2,1)S(1)}, bf16[4,3584,24]{1,2,0:T(8,128)(2,1)}, u32[]{:S(2)}) copy-start(bf16[4,3584,24]{1,2,0:T(8,128)(2,1)} %param.14) | copy-start | bytes 2064388
Sparse Core Ops, SparseCore 0:
  9.1 150.4 all-gather.7
  161.4 130.7 all-gather.9
  305.4 268.8 all-gather.5
where the time goes:
time: 584 us; the launch traced here: 583 us
  waiting for transfers between devices  484 us (83%)
  matrix products  30.1 us (5%)
  other arithmetic  23.1 us (4%)
  between operations  16.2 us (3%)
  local copies, waits for them, and re-layouts  13.2 us (2%)
  blocking collectives  13.1 us (2%)
    all_gather x1, waiting for transfers between devices, on_device(): shard_piece = lax.all_gather(stacked, 'seq', axis=1, tiled=True)  265 us
    all_gather x2, waiting for transfers between devices, latent_of(): lax.all_gather(w_latent[layer_index], 'seq', axis=0, tiled=True)  217 us
    dot_general x2, matrix products, latent_of(): jnp.dot(hidden, lax.all_gather(w_latent[layer_index], 'seq', axis=0, tile...  15 us
    all_to_all x3, blocking collectives, sent_to_all(): return lax.all_to_all(copies, axis, split_axis=0, concat_axis=0, tiled=True)  13.1 us
    reduce_sum x2, other arithmetic, coefficients(): jnp.sum(jnp.square(flattened.astype(jnp.float32)), axis=1)  12 us
  transfers between devices with their start and end apart: 4, of which 4 were waited for; matrix products, arithmetic and copies ran while one was open for 9% of the time, Pallas kernels for 0%

commit v1 on v0

--- a/solution.py
+++ b/solution.py
@@ -9,6 +9,11 @@
 SINK = 20
 EPSILON = 1e-06
 THETA = 10000.0
+
+
+def all_by_exchange(block, name, dim):
+    stack = jnp.stack([block] * lax.axis_size(name))
+    return jnp.concatenate(lax.all_to_all(stack, name, 0, 0), axis=dim)
 
 
 def sent_to_all(x, axis):
@@ -113,7 +118,7 @@
     def latent_of(hidden, layer_index):
         partial_value = jnp.dot(
             hidden,
-            lax.all_gather(w_latent[layer_index], "seq", axis=0, tiled=True),
+            all_by_exchange(w_latent[layer_index], "seq", 0),
             preferred_element_type=jnp.float32,
         )
         summed = taken_together(partial_value, "pd")

time: 584 us -> 1210 us (2.07)
  waiting for transfers between devices: 484 us -> 1060 us
  starting transfers between devices: 3.43 us -> 57.4 us
    all_to_all x0 -> x2, waiting for transfers between devices: none -> 779 us  [all_by_exchange(): return jnp.concatenate(lax.all_to_all(stack, name, 0, 0), axis=dim)]
    all_gather x2 -> x0, waiting for transfers between devices: 217 us -> none  [latent_of(): lax.all_gather(w_latent[layer_index], 'seq', axis=0, tiled=True)]
    all_to_all x0 -> x2, starting transfers between devices: none -> 54.1 us  [all_by_exchange(): return jnp.concatenate(lax.all_to_all(stack, name, 0, 0), axis=dim)]
  transfers between devices with their start and end apart: 4 -> 4, of which waited for: 4 -> 4; matrix products, arithmetic and copies ran while one was open for 9% -> 1% of each run, Pallas kernels for 0% -> 0%
where the time goes in v1:
time: 1210 us
  waiting for transfers between devices  1060 us (88%)
  starting transfers between devices  57.4 us (5%)
  other arithmetic  26.3 us (2%)
  matrix products  22.4 us (2%)
  between operations  16.5 us (1%)
  local copies, waits for them, and re-layouts  15.1 us (1%)
  blocking collectives  13.1 us (1%)
    all_to_all x2, waiting for transfers between devices, all_by_exchange(): return jnp.concatenate(lax.all_to_all(stack, name, 0, 0), axis=dim)  779 us
    all_gather x1, waiting for transfers between devices, on_device(): shard_piece = lax.all_gather(stacked, 'seq', axis=1, tiled=True)  274 us
    all_to_all x2, starting transfers between devices, all_by_exchange(): return jnp.concatenate(lax.all_to_all(stack, name, 0, 0), axis=dim)  54.1 us
  transfers between devices with their start and end apart: 4, of which 4 were waited for; matrix products, arithmetic and copies ran while one was open for 1% of the time, Pallas kernels for 0%

profile of v1, /device:TPU:38, one launch (start us, length us, event | category | flops | bytes accessed | tf_op | source)
XLA Modules:
  0.0 1206.5 jit_solution(18174721276216569019)
XLA Ops:
  6.6 8.1 multiply_reduce_fusion.1
  14.7 2.1 convolution_bitcast_fusion
  16.8 0.1 reshape.338
  16.9 0.6 broadcast_in_dim.23
  17.6 3.3 all-to-all-start
  20.9 1.3 all-to-all-done
  22.3 2.4 stack.31
  24.7 32.9 %all-to-all-start.1 = ((bf16[32,112,576]{2,1,0:T(8,128)(2,1)}), bf16[32,112,576]{2,1,0:T(8,128)(2,1)}, u32[]{:S(2)}, u32[]{:S(2)}) async-start(bf16[32,112,576]{2,1,0:T(8,128)(2,1)} %stack.31), calls=%async_computation.1 | async-start | bytes 9175040 | tf_op jit(solution)/shard_map/all_to_all | solution.py:16
  57.6 7.4 copy.65
  64.9 0.1 reduce_sum.111
  65.0 0.1 reshape.339
  65.4 1.7 while.10
  67.2 385.9 %all-to-all-done.1 = bf16[32,112,576]{2,1,0:T(8,128)(2,1)} async-done(((bf16[32,112,576]{2,1,0:T(8,128)(2,1)}), bf16[32,112,576]{2,1,0:T(8,128)(2,1)}, u32[]{:S(2)}, u32[]{:S(2)}) %all-to-all-start.1) | async-done | bytes 4128800 | tf_op jit(solution)/shard_map/all_to_all | solution.py:16
  453.1 8.4 fusion.44
  461.5 0.1 broadcast_in_dim.24
  461.6 4.7 all_to_all.32
  466.3 0.1 reduce_sum.112
  466.4 0.1 multiply_reduce_fusion.3
  466.5 3.3 fusion.100
  469.8 5.7 fusion.56
  475.6 3.7 fusion.57
  479.3 1.8 multiply_reduce_fusion
  481.1 2.0 fusion.59
  483.1 0.1 reshape.341
  483.3 3.7 all_to_all.33
  487.0 2.5 stack.37
  489.5 21.2 %all-to-all-start.4 = ((bf16[32,112,576]{2,1,0:T(8,128)(2,1)}), bf16[32,112,576]{2,1,0:T(8,128)(2,1)}, u32[]{:S(2)}, u32[]{:S(2)}) async-start(bf16[32,112,576]{2,1,0:T(8,128)(2,1)} %stack.37), calls=%async_computation.4 | async-start | bytes 9175040 | tf_op jit(solution)/shard_map/all_to_all | solution.py:16
  511.5 0.2 fusion.92
  511.7 0.1 compare_bitcast_fusion
  511.9 0.1 reshape.342
  512.1 0.1 add_divide_fusion
  512.2 0.1 fusion.101
  512.3 393.6 %all-to-all-done.4 = bf16[32,112,576]{2,1,0:T(8,128)(2,1)} async-done(((bf16[32,112,576]{2,1,0:T(8,128)(2,1)}), bf16[32,112,576]{2,1,0:T(8,128)(2,1)}, u32[]{:S(2)}, u32[]{:S(2)}) %all-to-all-start.4) | async-done | bytes 4128800 | tf_op jit(solution)/shard_map/all_to_all | solution.py:16
  905.9 6.6 fusion.41
  912.5 0.1 broadcast_in_dim.27
  912.6 4.7 all_to_all.34
  917.3 0.1 reduce_sum.116
  917.4 0.1 multiply_reduce_fusion.2
  917.5 0.1 fusion.64
  917.6 0.2 fusion.84
  917.9 0.1 maximum_select_fusion
  918.0 0.9 pad_maximum_fusion.4
  918.9 0.7 fusion.97
  920.4 0.6 gather_fusion
  921.0 0.6 fusion.111
  922.9 274.4 %all-gather.2.cloned.1.call-done = bf16[2,8192,576]{1,2,0:T(8,128)(2,1)} async-done(((bf16[2,256,576]{1,2,0:T(8,128)(2,1)}), bf16[2,8192,576]{1,2,0:T(8,128)(2,1)}) %all-gather.2.cloned.1.call-update) | async-done | bytes 18874384 | tf_op jit(solution)/shard_map/all_gather | solution.py:152
  1197.3 1.5 dynamic-slice_select_fusion.1
  1198.8 0.9 pad_maximum_fusion.5
  (122 shorter events, 2.0 us)
Async XLA Ops:
  6.5 8.1 copy-start
  6.6 8.1 copy-start.3
  14.7 6.2 copy-start.7
  17.6 4.7 all-to-all-start
  24.7 428.4 %all-to-all-start.1 = ((bf16[32,112,576]{2,1,0:T(8,128)(2,1)}), bf16[32,112,576]{2,1,0:T(8,128)(2,1)}, u32[]{:S(2)}, u32[]{:S(2)}) async-start(bf16[32,112,576]{2,1,0:T(8,128)(2,1)} %stack.31), calls=%async_computation.1 | async-start | bytes 9175040 | tf_op jit(solution)/shard_map/all_to_all | solution.py:16
  57.5 7.7 copy-start.9
  57.6 7.8 copy-start.8
  469.8 5.8 slice-start
  469.8 5.8 slice-start.1
  475.5 5.5 copy-start.4
  479.2 1.8 copy-start.5
  479.3 1.9 copy-start.6
  479.3 1.8 copy-start.11
  489.5 22.0 %copy-start.2 = (s32[64]{0:T(128)S(1)}, s32[64]{0:T(128)}, u32[]{:S(2)}) copy-start(s32[64]{0:T(128)} %param.21) | copy-start | bytes 772
  489.5 22.6 %copy-start.10 = (f32[4]{0:T(128)S(1)}, f32[4]{0:T(128)}, u32[]{:S(2)}) copy-start(f32[4]{0:T(128)} %param.17) | copy-start | bytes 52
  489.5 416.4 %all-to-all-start.4 = ((bf16[32,112,576]{2,1,0:T(8,128)(2,1)}), bf16[32,112,576]{2,1,0:T(8,128)(2,1)}, u32[]{:S(2)}, u32[]{:S(2)}) async-start(bf16[32,112,576]{2,1,0:T(8,128)(2,1)} %stack.37), calls=%async_computation.4 | async-start | bytes 9175040 | tf_op jit(solution)/shard_map/all_to_all | solution.py:16
  510.7 686.5 %all-gather.2.cloned.1.call-start = ((), (), s32[]{:S(2)}) async-start(), calls=%async_computation.6 | async-start | bytes 19464192 | tf_op jit(solution)/shard_map/all_gather | solution.py:152
  917.3 1.6 copy-start.12
  917.3 282.4 %copy-start.1 = (bf16[4,3584,24]{1,2,0:T(8,128)(2,1)S(1)}, bf16[4,3584,24]{1,2,0:T(8,128)(2,1)}, u32[]{:S(2)}) copy-start(bf16[4,3584,24]{1,2,0:T(8,128)(2,1)} %param.14) | copy-start | bytes 2064388
Sparse Core Ops, SparseCore 0:
  919.0 278.1 all-gather.1
